TPU v7x, 32 devices: a whole 2x2x4 slice. The times are simulated.
32 devices in a mesh: unit: 2 (over core), block: 4 (over z), lane: 4 (over y, x).
Axes of the slice: x: 2, y: 2, z: 4, core: 2. Of those that a mesh axis runs over, the one named last changes fastest.
Arguments:
- image_rows: bfloat16 [2048, 512], P(('unit', 'block', 'lane')), parts along dimension 0, may hold values from -6 to 6, as said below
- text_rows: bfloat16 [2048, 512], P(('unit', 'block', 'lane')), parts along dimension 0, may hold values from -6 to 6, as said below
Outputs:
- image_loss: float32 [2048], P(('unit', 'block', 'lane')), parts along dimension 0
- text_loss: float32 [2048], P(('unit', 'block', 'lane')), parts along dimension 0
- image_grad: float32 [2048, 512], P(('unit', 'block', 'lane')), parts along dimension 0
- text_grad: float32 [2048, 512], P(('unit', 'block', 'lane')), parts along dimension 0
There are 2 independent parts, one for each index of `unit`. A program takes and returns all parts, laid end to end along the dimension named above; each array names one. Nothing has to cross between parts.
Inputs may be any that keep to these rules, and one draw needn't show every extreme that they name: image_rows holds numbers from -6 to 6. text_rows holds numbers from -6 to 6.
All inputs are finite; a program needn't handle non-finite values.
Results may differ from a plain program's by a relative error of at most 0.0035.
Values may be sent and summed in bfloat16 or wider, within the bound.
A program may use at most 64 MiB of HBM per device.

v0:
```python
import jax
import jax.numpy as jnp
from jax import lax
from jax.sharding import PartitionSpec as P


def unit_rows(values):
    wide = values.astype(jnp.float32)
    return (wide * lax.rsqrt(jnp.sum(wide * wide, axis=-1, keepdims=True) + 1e-06)).astype(
        jnp.bfloat16
    )


def body(image_rows, text_rows):
    image_unit, text_unit = (unit_rows(image_rows), unit_rows(text_rows))
    rows_here = image_rows.shape[0]
    matched = 12.0 * jnp.sum(image_unit.astype(jnp.float32) * text_unit.astype(jnp.float32), axis=1)
    my_images = lax.all_gather(image_unit, "lane", axis=0, tiled=True)
    my_texts = lax.all_gather(text_unit, "block", axis=0, tiled=True)
    power = jnp.exp(12.0 * jnp.dot(my_images, my_texts.T, preferred_element_type=jnp.float32))
    row_block = lax.psum(jnp.sum(power, axis=1), "lane")
    column_block = lax.psum(jnp.sum(power, axis=0), "block")
    row_sum = lax.dynamic_slice_in_dim(row_block, lax.axis_index("lane") * rows_here, rows_here)
    column_sum = lax.dynamic_slice_in_dim(
        column_block, lax.axis_index("block") * rows_here, rows_here
    )
    image_ids = lax.axis_index("block") * my_images.shape[0] + jnp.arange(my_images.shape[0])
    text_ids = (
        jnp.arange(lax.axis_size("block"))[:, None] * (lax.axis_size("lane") * rows_here)
        + lax.axis_index("lane") * rows_here
        + jnp.arange(rows_here)[None, :]
    ).reshape(-1)
    same = image_ids[:, None] == text_ids[None, :]
    pull = (
        power / row_block[:, None] + power / column_block[None, :] - jnp.where(same, 2.0, 0.0)
    ).astype(jnp.bfloat16)

    def image_term():
        part = lax.slice_in_dim(pull, 0, rows_here * lax.axis_size("lane"), axis=0)
        return jnp.dot(part, my_texts, preferred_element_type=jnp.float32)

    def text_term():
        part = lax.slice_in_dim(pull, 0, rows_here * lax.axis_size("block"), axis=1)
        return jnp.dot(part.T, my_images, preferred_element_type=jnp.float32)

    image_grad = lax.psum_scatter(image_term(), "lane", scatter_dimension=0, tiled=True)
    text_grad = lax.psum_scatter(text_term(), "block", scatter_dimension=0, tiled=True)
    image_loss, text_loss = (jnp.log(row_sum) - matched, jnp.log(column_sum) - matched)
    return (image_loss, text_loss, image_grad, text_grad)


def solution(mesh):
    in_specs = (P(("unit", "block", "lane"), None), P(("unit", "block", "lane"), None))
    out_specs = (
        P(("unit", "block", "lane")),
        P(("unit", "block", "lane")),
        P(("unit", "block", "lane"), None),
        P(("unit", "block", "lane"), None),
    )
    return jax.shard_map(body, mesh=mesh, in_specs=in_specs, out_specs=out_specs, check_vma=False)
```

profile of v0, /device:TPU:0, one launch (start us, length us, event | category | flops | bytes accessed | tf_op | source)
XLA Modules:
  0.0 108.9 jit_solution(18258325936602194781)
XLA Ops:
  7.2 0.0 copy-start
  7.2 0.0 reduce-scatter.5.cloned.1.call-start
  7.2 0.0 copy-start.1
  7.2 1.0 fusion.1
  8.3 0.0 copy-done
  8.3 0.1 fusion.3
  8.4 0.1 iota_add_fusion
  8.5 0.1 add.86
  8.6 0.0 copy-done.1
  8.6 0.2 multiply_reduce_fusion
  8.8 15.5 %all_gather.7 = bf16[256,512]{1,0:T(8,128)(2,1)S(1)} all-gather(bf16[64,512]{1,0:T(8,128)(2,1)S(1)} %get-tuple-element.7), channel_id=1, replica_groups=mesh['unit'=2,'block'=4,'lane'=4] {'block'}, dimensions={0}, use_global_device_ids=true | all-gather | bytes 327680 | tf_op jit(solution)/shard_map/all_gather | solution.py:19
  24.3 9.2 %all_gather.6 = bf16[256,512]{1,0:T(8,128)(2,1)S(1)} all-gather(bf16[64,512]{1,0:T(8,128)(2,1)S(1)} %get-tuple-element.8), channel_id=1, replica_groups=mesh['unit'=2,'block'=4,'lane'=4] {'lane'}, dimensions={0}, use_global_device_ids=true | all-gather | bytes 327680 | tf_op jit(solution)/shard_map/all_gather | solution.py:18
  33.5 0.4 fusion.5
  33.8 12.2 %psum.15 = f32[256]{0:T(256)S(1)} all-reduce(f32[256]{0:T(256)S(1)} %get-tuple-element.4), channel_id=1, replica_groups=mesh['unit'=2,'block'=4,'lane'=4] {'block'}, use_global_device_ids=true, to_apply=%region_6.0 | all-reduce | flops 256 | bytes 2048 | tf_op jit(solution)/shard_map/psum | solution.py:22
  46.1 8.9 %psum.14 = f32[256]{0:T(256)S(1)} all-reduce(f32[256]{0:T(256)S(1)} %get-tuple-element.5), channel_id=1, replica_groups=mesh['unit'=2,'block'=4,'lane'=4] {'lane'}, use_global_device_ids=true, to_apply=%region_3.0 | all-reduce | flops 256 | bytes 2048 | tf_op jit(solution)/shard_map/psum | solution.py:21
  55.0 0.1 subtract_convert_fusion
  55.2 1.1 fusion.9
  56.2 0.0 reduce-scatter.5.cloned.1.call-update
  56.2 0.0 reduce-scatter.3.cloned.1.call-start
  56.3 1.0 fusion.8
  57.3 0.0 reduce-scatter.3.cloned.1.call-update
  57.3 0.6 log_subtract_fusion
  57.9 17.4 %reduce-scatter.5.cloned.1.call-done = f32[64,512]{1,0:T(8,128)} async-done(((f32[256,512]{1,0:T(8,128)}), f32[64,512]{1,0:T(8,128)}) %reduce-scatter.5.cloned.1.call-update) | async-done | bytes 131088 | tf_op jit(solution)/shard_map/reduce_scatter | solution.py:47
  75.3 26.8 %reduce-scatter.3.cloned.1.call-done = f32[64,512]{1,0:T(8,128)} async-done(((f32[256,512]{1,0:T(8,128)}), f32[64,512]{1,0:T(8,128)}) %reduce-scatter.3.cloned.1.call-update) | async-done | bytes 131088 | tf_op jit(solution)/shard_map/reduce_scatter | solution.py:46
  (3 shorter events, 0.0 us)
Async XLA Ops:
  7.2 1.1 %copy-start = (bf16[64,512]{1,0:T(8,128)(2,1)S(1)}, bf16[64,512]{1,0:T(8,128)(2,1)}, u32[]{:S(2)}) copy-start(bf16[64,512]{1,0:T(8,128)(2,1)} %param.3) | copy-start | bytes 196612
  7.2 68.1 %reduce-scatter.5.cloned.1.call-start = ((), (), s32[]{:S(2)}) async-start(), calls=%async_computation.3 | async-start | bytes 655360 | tf_op jit(solution)/shard_map/reduce_scatter | solution.py:47
  7.2 1.3 %copy-start.1 = (bf16[64,512]{1,0:T(8,128)(2,1)S(1)}, bf16[64,512]{1,0:T(8,128)(2,1)}, u32[]{:S(2)}) copy-start(bf16[64,512]{1,0:T(8,128)(2,1)} %param.2) | copy-start | bytes 196612
  56.2 45.8 %reduce-scatter.3.cloned.1.call-start = ((), (), s32[]{:S(2)}) async-start(), calls=%async_computation.2 | async-start | bytes 655360 | tf_op jit(solution)/shard_map/reduce_scatter | solution.py:46
Sparse Core Ops, SparseCore 0:
  56.4 18.8 reduce-scatter.4
  78.7 23.3 reduce-scatter.2
where the time goes:
time: 109 us
  blocking collectives  45.9 us (42%)
  waiting for transfers between devices  44.2 us (41%)
  between operations  14.1 us (13%)
  matrix products  2.43 us (2%)
  other arithmetic  2.15 us (2%)
    reduce_scatter x1, waiting for transfers between devices, body(): lax.psum_scatter(image_term(), 'lane', scatter_dimension=0, tiled=True)  26.8 us
    reduce_scatter x1, waiting for transfers between devices, body(): lax.psum_scatter(text_term(), 'block', scatter_dimension=0, tiled=True)  17.4 us
    all_gather x1, blocking collectives, body(): my_texts = lax.all_gather(text_unit, 'block', axis=0, tiled=True)  15.5 us
    psum x1, blocking collectives, body(): column_block = lax.psum(jnp.sum(power, axis=0), 'block')  12.2 us
    all_gather x1, blocking collectives, body(): my_images = lax.all_gather(image_unit, 'lane', axis=0, tiled=True)  9.19 us
    psum x1, blocking collectives, body(): row_block = lax.psum(jnp.sum(power, axis=1), 'lane')  8.94 us
  transfers between devices with their start and end apart: 2, of which 2 were waited for; matrix products, arithmetic and copies ran while one was open for 1% of the time, Pallas kernels for 0%

commit v1 on v0

v1 whole, which is shorter than its diff:
```python
import functools

import jax
import jax.numpy as jnp
from jax import lax
from jax.experimental import pallas as pl
from jax.experimental.pallas import tpu as pltpu
from jax.sharding import PartitionSpec as P

NT = (((1,), (1,)), ((), ()))


def unit_rows(values):
    wide = values.astype(jnp.float32)
    scale = lax.rsqrt(jnp.sum(wide * wide, axis=-1, keepdims=True) + 1e-06)
    return (wide * scale).astype(jnp.bfloat16)


def upright(row):
    return jnp.transpose(jnp.broadcast_to(row, (8, row.shape[1])))[:, :1]


def own_piece(row, pieces, mine):
    size = row.shape[1] // pieces
    return sum(
        jnp.where(mine == piece, row[:, piece * size : (piece + 1) * size], 0.0)
        for piece in range(pieces)
    )


def kernel(
    lanes,
    blocks,
    group,
    image_hbm,
    text_hbm,
    image_loss,
    text_loss,
    image_grad,
    text_grad,
    image_raw,
    text_raw,
    images,
    texts,
    power,
    power_t,
    row_mine,
    row_in,
    col_mine,
    col_in,
    image_acc,
    image_out,
    image_in,
    text_out,
    text_in,
    text_own,
    load_sem,
    send_image,
    recv_image,
    send_text,
    recv_text,
    send_row,
    recv_row,
    send_col,
    recv_col,
    send_ig,
    recv_ig,
    send_tg,
    recv_tg,
):
    lane, block = lax.axis_index("lane"), lax.axis_index("block")
    rows = image_raw.shape[0]
    images_n, texts_n = lanes * rows, blocks * rows
    groups = texts_n // group
    per_group = group // rows

    loads = [
        pltpu.make_async_copy(image_hbm, image_raw, load_sem.at[0]),
        pltpu.make_async_copy(text_hbm, text_raw, load_sem.at[1]),
    ]
    for load in loads:
        load.start()
    barrier = pltpu.get_barrier_semaphore()
    for k in range(1, blocks):
        pl.semaphore_signal(barrier, inc=1, device_id={"block": lax.rem(block + k, blocks)})
    for k in range(1, lanes):
        pl.semaphore_signal(barrier, inc=1, device_id={"lane": lax.rem(lane + k, lanes)})

    my_image = pl.ds(pl.multiple_of(lane * rows, rows), rows)
    my_text = pl.ds(pl.multiple_of(block * rows, rows), rows)
    loads[1].wait()
    texts[my_text, :] = unit_rows(text_raw[...])
    loads[0].wait()
    images[my_image, :] = unit_rows(image_raw[...])
    pl.semaphore_wait(barrier, lanes + blocks - 2)

    def to_block(k, src, dst, send, recv):
        return pltpu.make_async_remote_copy(
            src_ref=src,
            dst_ref=dst,
            send_sem=send.at[k - 1],
            recv_sem=recv.at[k - 1],
            device_id={"block": lax.rem(block + k, blocks)},
        )

    def to_lane(k, src, dst, send, recv):
        return pltpu.make_async_remote_copy(
            src_ref=src,
            dst_ref=dst,
            send_sem=send.at[k - 1],
            recv_sem=recv.at[k - 1],
            device_id={"lane": lax.rem(lane + k, lanes)},
        )

    text_copies = [
        to_block(k, texts.at[my_text], texts.at[my_text], send_text, recv_text)
        for k in range(1, blocks)
    ]
    image_copies = [
        to_lane(k, images.at[my_image], images.at[my_image], send_image, recv_image)
        for k in range(1, lanes)
    ]
    for copy in text_copies + image_copies:
        copy.start()

    pair = 12.0 * lax.dot_general(
        images[my_image, :], texts[my_text, :], NT, preferred_element_type=jnp.float32
    )
    eye = lax.broadcasted_iota(jnp.int32, (rows, rows), 0) == lax.broadcasted_iota(
        jnp.int32, (rows, rows), 1
    )
    matched = jnp.sum(jnp.where(eye, pair, 0.0), axis=0, keepdims=True)

    for copy in image_copies + text_copies:
        copy.wait_recv()

    def over_groups(step, start):
        if groups == 1:
            return step(0, start)
        return lax.fori_loop(0, groups, step, start)

    def group_rows(g):
        return pl.ds(g * group if groups == 1 else pl.multiple_of(g * group, group), group)

    def power_step(g, row_sum):
        some = texts[group_rows(g), :]
        p = jnp.exp(12.0 * lax.dot_general(images[...], some, NT, preferred_element_type=jnp.float32))
        q = jnp.exp(12.0 * lax.dot_general(some, images[...], NT, preferred_element_type=jnp.float32))
        power[g] = p
        power_t[g] = q
        col_mine[g] = jnp.sum(p, axis=0, keepdims=True)
        return row_sum + jnp.sum(q, axis=0, keepdims=True)

    row_mine[...] = over_groups(power_step, jnp.zeros((1, images_n), jnp.float32))
    sum_copies = [
        to_block(k, col_mine, col_in.at[k - 1], send_col, recv_col) for k in range(1, blocks)
    ] + [to_lane(k, row_mine, row_in.at[k - 1], send_row, recv_row) for k in range(1, lanes)]
    for copy in sum_copies:
        copy.start()
    for copy in sum_copies:
        copy.wait_recv()

    row_sum = row_mine[...]
    for k in range(1, lanes):
        row_sum = row_sum + row_in[k - 1]
    row_inv = 1.0 / row_sum
    row_inv_up = upright(row_inv)
    image_loss[...] = jnp.log(own_piece(row_sum, lanes, lane)) - matched

    def col_total(g):
        total = col_mine[g]
        for k in range(1, blocks):
            total = total + col_in[k - 1, g]
        return total

    image_acc[...] = jnp.zeros_like(image_acc)

    def grad_step(g, own_col):
        total = col_total(g)
        col_inv = 1.0 / total
        col_inv_up = upright(col_inv)
        first = block - g * per_group
        ids_t = lax.broadcasted_iota(jnp.int32, (group, images_n), 0) - first * rows
        ids_i = lax.broadcasted_iota(jnp.int32, (group, images_n), 1) - lane * rows
        same_t = (ids_t == ids_i) & (ids_i >= 0) & (ids_i < rows)
        pull_t = (power_t[g] * (row_inv + col_inv_up) - jnp.where(same_t, 2.0, 0.0)).astype(
            jnp.bfloat16
        )
        part = jnp.dot(pull_t, images[...], preferred_element_type=jnp.float32)
        text_own[group_rows(g), :] = part
        text_out[group_rows(g), :] = part.astype(jnp.bfloat16)
        ids_i = lax.broadcasted_iota(jnp.int32, (images_n, group), 0) - lane * rows
        ids_t = lax.broadcasted_iota(jnp.int32, (images_n, group), 1) - first * rows
        same = (ids_t == ids_i) & (ids_i >= 0) & (ids_i < rows)
        pull = (power[g] * (row_inv_up + col_inv) - jnp.where(same, 2.0, 0.0)).astype(jnp.bfloat16)
        image_acc[...] += jnp.dot(
            pull, texts[group_rows(g), :], preferred_element_type=jnp.float32
        )
        return own_col + own_piece(total, per_group, first)

    own_col = over_groups(grad_step, jnp.zeros((1, rows), jnp.float32))
    image_out[...] = image_acc[...].astype(jnp.bfloat16)

    def there(index, count, k):
        return pl.ds(pl.multiple_of(lax.rem(index + k, count) * rows, rows), rows)

    tg_copies = [
        to_block(k, text_out.at[there(block, blocks, k)], text_in.at[k - 1], send_tg, recv_tg)
        for k in range(1, blocks)
    ]
    ig_copies = [
        to_lane(k, image_out.at[there(lane, lanes, k)], image_in.at[k - 1], send_ig, recv_ig)
        for k in range(1, lanes)
    ]
    for copy in tg_copies + ig_copies:
        copy.start()
    text_loss[...] = jnp.log(own_col) - matched
    for copy in ig_copies:
        copy.wait_recv()
    grad = image_acc[my_image, :]
    for k in range(1, lanes):
        grad = grad + image_in[k - 1].astype(jnp.float32)
    image_grad[...] = grad
    for copy in tg_copies:
        copy.wait_recv()
    grad = text_own[my_text, :]
    for k in range(1, blocks):
        grad = grad + text_in[k - 1].astype(jnp.float32)
    text_grad[...] = grad
    for copy in text_copies + image_copies + sum_copies + tg_copies + ig_copies:
        copy.wait_send()


def solution(mesh):
    lanes, blocks = mesh.shape["lane"], mesh.shape["block"]

    def body(image_rows, text_rows):
        rows, width = image_rows.shape
        images_n, texts_n = lanes * rows, blocks * rows
        group = rows * next(c for c in (4, 2, 1) if blocks % c == 0)
        groups = texts_n // group
        f32, bf16 = jnp.float32, jnp.bfloat16
        sems = [pltpu.SemaphoreType.DMA((2,))]
        for count in (lanes, blocks, lanes, blocks, lanes, blocks):
            sems += [pltpu.SemaphoreType.DMA((max(count - 1, 1),))] * 2
        image_loss, text_loss, image_grad, text_grad = pl.pallas_call(
            functools.partial(kernel, lanes, blocks, group),
            out_shape=(
                jax.ShapeDtypeStruct((1, rows), f32),
                jax.ShapeDtypeStruct((1, rows), f32),
                jax.ShapeDtypeStruct((rows, width), f32),
                jax.ShapeDtypeStruct((rows, width), f32),
            ),
            in_specs=[pl.BlockSpec(memory_space=pl.ANY)] * 2,
            out_specs=[pl.BlockSpec(memory_space=pltpu.VMEM)] * 4,
            scratch_shapes=[
                pltpu.VMEM((rows, width), bf16),
                pltpu.VMEM((rows, width), bf16),
                pltpu.VMEM((images_n, width), bf16),
                pltpu.VMEM((texts_n, width), bf16),
                pltpu.VMEM((groups, images_n, group), f32),
                pltpu.VMEM((groups, group, images_n), f32),
                pltpu.VMEM((1, images_n), f32),
                pltpu.VMEM((max(lanes - 1, 1), 1, images_n), f32),
                pltpu.VMEM((groups, 1, group), f32),
                pltpu.VMEM((max(blocks - 1, 1), groups, 1, group), f32),
                pltpu.VMEM((images_n, width), f32),
                pltpu.VMEM((images_n, width), bf16),
                pltpu.VMEM((max(lanes - 1, 1), rows, width), bf16),
                pltpu.VMEM((texts_n, width), bf16),
                pltpu.VMEM((max(blocks - 1, 1), rows, width), bf16),
                pltpu.VMEM((texts_n, width), f32),
            ]
            + sems,
            compiler_params=pltpu.CompilerParams(collective_id=0, has_side_effects=True),
        )(image_rows, text_rows)
        return (image_loss.reshape(rows), text_loss.reshape(rows), image_grad, text_grad)

    rows_spec = P(("unit", "block", "lane"), None)
    flat_spec = P(("unit", "block", "lane"))
    return jax.shard_map(
        body,
        mesh=mesh,
        in_specs=(rows_spec, rows_spec),
        out_specs=(flat_spec, flat_spec, rows_spec, rows_spec),
        check_vma=False,
    )
```

time: 109 us -> 27.7 us (0.25)
  blocking collectives: 45.9 us -> 0 us
  waiting for transfers between devices: 44.2 us -> 0 us
  Pallas kernels: 0 us -> 22.8 us
  between operations: 14.1 us -> 0.65 us
  local copies, waits for them, and re-layouts: 0.09 us -> 4.04 us
  matrix products: 2.43 us -> 0 us
  other arithmetic: 2.15 us -> 0 us
    reduce_scatter x2 -> x0, waiting for transfers between devices: 44.1 us -> none  [the longest x1 26.8 us: body(): lax.psum_scatter(image_term(), 'lane', scatter_dimension=0, tiled=True)]
    all_gather x2 -> x0, blocking collectives: 24.7 us -> none  [the longest x1 15.5 us: body(): my_texts = lax.all_gather(text_unit, 'block', axis=0, tiled=True)]
    pallas_call x0 -> x1, Pallas kernels: none -> 22.8 us  [body(): pl.pallas_call(functools.partial(kernel, lanes, blocks, group), out_shape...]
    psum x2 -> x0, blocking collectives: 21.2 us -> none  [the longest x1 12.2 us: body(): column_block = lax.psum(jnp.sum(power, axis=0), 'block')]
    unnamed x4 -> x10, local copies, waits for them, and re-layouts: 0.01 us -> 4.04 us
    dot_general x3 -> x0, matrix products: 2.43 us -> none  [the longest x1 1.06 us: text_term(): return jnp.dot(part.T, my_images, preferred_element_type=jnp.float32)]
    reduce_sum x3 -> x0, other arithmetic: 1.32 us -> none  [the longest x2 1.13 us: unit_rows(): jnp.sum(wide * wide, axis=-1, keepdims=True) + 1e-06]
  transfers between devices with their start and end apart: 2 -> 0, of which waited for: 2 -> 0; matrix products, arithmetic and copies ran while one was open for 1% -> 0% of each run, Pallas kernels for 0% -> 0%
where the time goes in v1:
time: 27.7 us; the launch traced here: 27.5 us
  Pallas kernels  22.8 us (82%)
  local copies, waits for them, and re-layouts  4.04 us (15%)
  between operations  0.65 us (2%)
    pallas_call x1, Pallas kernels, body(): pl.pallas_call(functools.partial(kernel, lanes, blocks, group), out_shape...  22.8 us
    unnamed x10, local copies, waits for them, and re-layouts  4.04 us

profile of v1, /device:TPU:0, one launch (start us, length us, event | category | flops | bytes accessed | tf_op | source)
XLA Modules:
  0.0 27.5 jit_solution(3704588707066291685)
XLA Ops:
  0.6 22.8 %shard_map.57 = (f32[1,64]{1,0:T(1,128)}, f32[1,64]{1,0:T(1,128)}, f32[64,512]{1,0:T(8,128)}, f32[64,512]{1,0:T(8,128)}) custom-call(bf16[64,512]{1,0:T(8,128)(2,1)} %image_hbm.1, bf16[64,512]{1,0:T(8,128)(2,1)} %text_hbm.1), custom_call_target="tpu_custom_call" | custom-call | tf_op jit(solution)/shard_map/pallas_call | solution.py:246
  23.5 0.0 copy-start.2
  23.5 0.7 %copy-done.2 = f32[1,64]{1,0:T(1,128)S(1)} copy-done((f32[1,64]{1,0:T(1,128)S(1)}, f32[1,64]{1,0:T(1,128)}, u32[]{:S(2)}) %copy-start.2) | copy-done | bytes 280
  24.2 0.0 copy-start.1
  24.2 0.5 %copy.10 = f32[64]{0:T(128)} copy(f32[64]{0:T(128)S(1)} %bitcast.3) | data formatting | bytes 512
  24.7 0.1 copy-done.1
  24.8 0.5 %copy.11 = f32[64]{0:T(128)} copy(f32[64]{0:T(128)S(1)} %bitcast.2) | data formatting | bytes 512
  25.3 0.0 copy-start
  25.3 1.6 %copy.12 = f32[64,512]{1,0:T(8,128)} copy(f32[64,512]{1,0:T(8,128)} %get-tuple-element.18) | data formatting | bytes 262144
  26.9 0.0 copy-done
  26.9 0.7 %copy.13 = f32[64,512]{1,0:T(8,128)} copy(f32[64,512]{1,0:T(8,128)S(1)} %copy-done) | data formatting | bytes 262144
Async XLA Ops:
  23.5 0.7 %copy-start.2 = (f32[1,64]{1,0:T(1,128)S(1)}, f32[1,64]{1,0:T(1,128)}, u32[]{:S(2)}) copy-start(f32[1,64]{1,0:T(1,128)} %get-tuple-element.8) | copy-start | bytes 772
  24.2 0.6 %copy-start.1 = (f32[1,64]{1,0:T(1,128)S(1)}, f32[1,64]{1,0:T(1,128)}, u32[]{:S(2)}) copy-start(f32[1,64]{1,0:T(1,128)} %get-tuple-element.9) | copy-start | bytes 772
  25.3 1.6 %copy-start = (f32[64,512]{1,0:T(8,128)S(1)}, f32[64,512]{1,0:T(8,128)}, u32[]{:S(2)}) copy-start(f32[64,512]{1,0:T(8,128)} %get-tuple-element.19) | copy-start | bytes 393220

commit v2 on v1

--- a/solution.py
+++ b/solution.py
@@ -231,6 +231,17 @@
         copy.wait_send()
 
 
+def place(*refs):
+    sem = refs[-1]
+    copies = [
+        pltpu.make_async_copy(refs[i], refs[i + 4], sem.at[i]) for i in (2, 3, 0, 1)
+    ]
+    for copy in copies:
+        copy.start()
+    for copy in copies:
+        copy.wait()
+
+
 def solution(mesh):
     lanes, blocks = mesh.shape["lane"], mesh.shape["block"]
 
@@ -240,6 +251,10 @@
         group = rows * next(c for c in (4, 2, 1) if blocks % c == 0)
         groups = texts_n // group
         f32, bf16 = jnp.float32, jnp.bfloat16
+        limit = 4 * (
+            images_n * texts_n * 8 + (images_n + texts_n) * width * 6 + rows * width * 64
+        )
+        limit = min(limit, 60 * 2**20)
         sems = [pltpu.SemaphoreType.DMA((2,))]
         for count in (lanes, blocks, lanes, blocks, lanes, blocks):
             sems += [pltpu.SemaphoreType.DMA((max(count - 1, 1),))] * 2
@@ -251,7 +266,7 @@
                 jax.ShapeDtypeStruct((rows, width), f32),
                 jax.ShapeDtypeStruct((rows, width), f32),
             ),
-            in_specs=[pl.BlockSpec(memory_space=pl.ANY)] * 2,
+            in_specs=[pl.BlockSpec(memory_space=pltpu.HBM)] * 2,
             out_specs=[pl.BlockSpec(memory_space=pltpu.VMEM)] * 4,
             scratch_shapes=[
                 pltpu.VMEM((rows, width), bf16),
@@ -272,8 +287,19 @@
                 pltpu.VMEM((texts_n, width), f32),
             ]
             + sems,
-            compiler_params=pltpu.CompilerParams(collective_id=0, has_side_effects=True),
+            compiler_params=pltpu.CompilerParams(
+                collective_id=0, has_side_effects=True, vmem_limit_bytes=limit
+            ),
         )(image_rows, text_rows)
+        results = (image_loss, text_loss, image_grad, text_grad)
+        image_loss, text_loss, image_grad, text_grad = pl.pallas_call(
+            place,
+            out_shape=tuple(jax.ShapeDtypeStruct(r.shape, r.dtype) for r in results),
+            in_specs=[pl.BlockSpec(memory_space=pltpu.VMEM)] * 4,
+            out_specs=[pl.BlockSpec(memory_space=pl.ANY)] * 4,
+            scratch_shapes=[pltpu.SemaphoreType.DMA((4,))],
+            compiler_params=pltpu.CompilerParams(vmem_limit_bytes=4 * rows * width * 8),
+        )(*results)
         return (image_loss.reshape(rows), text_loss.reshape(rows), image_grad, text_grad)
 
     rows_spec = P(("unit", "block", "lane"), None)

time: 27.7 us -> 25.5 us (0.921)
  local copies, waits for them, and re-layouts: 4.04 us -> 1.67 us
    unnamed x10 -> x4, local copies, waits for them, and re-layouts: 4.04 us -> 1.67 us
    pallas_call x0 -> x1, Pallas kernels: none -> 0.74 us  [body(): pl.pallas_call(place, out_shape=tuple((jax.ShapeDtypeStruct(r.shape, r.dt...]
    pallas_call x1, Pallas kernels: 22.8 us -> 22.2 us  [body(): pl.pallas_call(functools.partial(kernel, lanes, blocks, group), out_shape...]
where the time goes in v2:
time: 25.5 us; the launch traced here: 25.3 us
  Pallas kernels  23 us (90%)
  local copies, waits for them, and re-layouts  1.67 us (7%)
  between operations  0.65 us (3%)
    pallas_call x1, Pallas kernels, body(): pl.pallas_call(functools.partial(kernel, lanes, blocks, group), out_shape...  22.2 us
    unnamed x4, local copies, waits for them, and re-layouts  1.67 us
    pallas_call x1, Pallas kernels, body(): pl.pallas_call(place, out_shape=tuple((jax.ShapeDtypeStruct(r.shape, r.dt...  0.74 us

profile of v2, /device:TPU:0, one launch (start us, length us, event | category | flops | bytes accessed | tf_op | source)
XLA Modules:
  0.0 25.3 jit_solution(3177083016291066708)
XLA Ops:
  0.6 0.0 copy-start
  0.6 0.8 %copy-done = bf16[64,512]{1,0:T(8,128)(2,1)S(1)} copy-done((bf16[64,512]{1,0:T(8,128)(2,1)S(1)}, bf16[64,512]{1,0:T(8,128)(2,1)}, u32[]{:S(2)}) %copy-start) | copy-done | bytes 65560
  1.5 0.0 copy-start.1
  1.5 0.8 %copy-done.1 = bf16[64,512]{1,0:T(8,128)(2,1)S(1)} copy-done((bf16[64,512]{1,0:T(8,128)(2,1)S(1)}, bf16[64,512]{1,0:T(8,128)(2,1)}, u32[]{:S(2)}) %copy-start.1) | copy-done | bytes 65560
  2.3 22.2 %shard_map.57 = (f32[1,64]{1,0:T(1,128)S(1)}, f32[1,64]{1,0:T(1,128)S(1)}, f32[64,512]{1,0:T(8,128)S(1)}, f32[64,512]{1,0:T(8,128)S(1)}) custom-call(bf16[64,512]{1,0:T(8,128)(2,1)S(1)} %copy-done, bf16[64,512]{1,0:T(8,128)(2,1)S(1)} %copy-done.1), custom_call_target="tpu_custom_call" | custom-call | tf_op jit(solution)/shard_map/pallas_call | solution.py:261
  24.5 0.7 %shard_map.58 = (f32[1,64]{1,0:T(1,128)}, f32[1,64]{1,0:T(1,128)}, f32[64,512]{1,0:T(8,128)}, f32[64,512]{1,0:T(8,128)}) custom-call(f32[1,64]{1,0:T(1,128)S(1)} %get-tuple-element.12.refs_0_, f32[1,64]{1,0:T(1,128)S(1)} %get-tuple-element.13.refs_1_, f32[64,512]{1,0:T(8,128)S(1)} %get-tuple-element.14.refs_2_, f32[64,512]{1,0:T(8,128)S(1)} %get-tuple-element.15.refs_3_), custom_call_target="tpu_custom_call" | custom-call | tf_op jit(solution)/shard_map/pallas_call | solution.py:295
Async XLA Ops:
  0.6 0.8 %copy-start = (bf16[64,512]{1,0:T(8,128)(2,1)S(1)}, bf16[64,512]{1,0:T(8,128)(2,1)}, u32[]{:S(2)}) copy-start(bf16[64,512]{1,0:T(8,128)(2,1)} %image_hbm.1) | copy-start | bytes 196612
  1.5 0.8 %copy-start.1 = (bf16[64,512]{1,0:T(8,128)(2,1)S(1)}, bf16[64,512]{1,0:T(8,128)(2,1)}, u32[]{:S(2)}) copy-start(bf16[64,512]{1,0:T(8,128)(2,1)} %text_hbm.1) | copy-start | bytes 196612

commit v3 on v2

--- a/solution.py
+++ b/solution.py
@@ -290,7 +290,7 @@
             compiler_params=pltpu.CompilerParams(
                 collective_id=0, has_side_effects=True, vmem_limit_bytes=limit
             ),
-        )(image_rows, text_rows)
+        )(*(pltpu.with_memory_space_constraint(x, pltpu.HBM) for x in (image_rows, text_rows)))
         results = (image_loss, text_loss, image_grad, text_grad)
         image_loss, text_loss, image_grad, text_grad = pl.pallas_call(
             place,

time: 25.5 us -> 23.7 us (0.929)
  local copies, waits for them, and re-layouts: 1.67 us -> 0 us
    unnamed x4 -> x0, local copies, waits for them, and re-layouts: 1.67 us -> none
where the time goes in v3:
time: 23.7 us; the launch traced here: 23.5 us
  Pallas kernels  22.9 us (97%)
  between operations  0.64 us (3%)
    pallas_call x1, Pallas kernels, body(): pl.pallas_call(functools.partial(kernel, lanes, blocks, group), out_shape...  22.1 us
    pallas_call x1, Pallas kernels, body(): pl.pallas_call(place, out_shape=tuple((jax.ShapeDtypeStruct(r.shape, r.dt...  0.74 us

profile of v3, /device:TPU:0, one launch (start us, length us, event | category | flops | bytes accessed | tf_op | source)
XLA Modules:
  0.0 23.5 jit_solution(13565316382683911342)
XLA Ops:
  0.6 22.1 %shard_map.57 = (f32[1,64]{1,0:T(1,128)S(1)}, f32[1,64]{1,0:T(1,128)S(1)}, f32[64,512]{1,0:T(8,128)S(1)}, f32[64,512]{1,0:T(8,128)S(1)}) custom-call(bf16[64,512]{1,0:T(8,128)(2,1)} %image_hbm.1, bf16[64,512]{1,0:T(8,128)(2,1)} %text_hbm.1), custom_call_target="tpu_custom_call" | custom-call | tf_op jit(solution)/shard_map/pallas_call | solution.py:261
  22.8 0.7 %shard_map.58 = (f32[1,64]{1,0:T(1,128)}, f32[1,64]{1,0:T(1,128)}, f32[64,512]{1,0:T(8,128)}, f32[64,512]{1,0:T(8,128)}) custom-call(f32[1,64]{1,0:T(1,128)S(1)} %get-tuple-element.12.refs_0_, f32[1,64]{1,0:T(1,128)S(1)} %get-tuple-element.13.refs_1_, f32[64,512]{1,0:T(8,128)S(1)} %get-tuple-element.14.refs_2_, f32[64,512]{1,0:T(8,128)S(1)} %get-tuple-element.15.refs_3_), custom_call_target="tpu_custom_call" | custom-call | tf_op jit(solution)/shard_map/pallas_call | solution.py:295

commit v4 on v3

--- a/solution.py
+++ b/solution.py
@@ -18,6 +18,10 @@
 
 def upright(row):
     return jnp.transpose(jnp.broadcast_to(row, (8, row.shape[1])))[:, :1]
+
+
+def both_ways(count):
+    return sorted(range(1, count), key=lambda k: (min(k, count - k), k))
 
 
 def own_piece(row, pieces, mine):
@@ -90,8 +94,6 @@
     my_text = pl.ds(pl.multiple_of(block * rows, rows), rows)
     loads[1].wait()
     texts[my_text, :] = unit_rows(text_raw[...])
-    loads[0].wait()
-    images[my_image, :] = unit_rows(image_raw[...])
     pl.semaphore_wait(barrier, lanes + blocks - 2)
 
     def to_block(k, src, dst, send, recv):
@@ -114,13 +116,17 @@
 
     text_copies = [
         to_block(k, texts.at[my_text], texts.at[my_text], send_text, recv_text)
-        for k in range(1, blocks)
-    ]
+        for k in both_ways(blocks)
+    ]
+    for copy in text_copies:
+        copy.start()
+    loads[0].wait()
+    images[my_image, :] = unit_rows(image_raw[...])
     image_copies = [
         to_lane(k, images.at[my_image], images.at[my_image], send_image, recv_image)
         for k in range(1, lanes)
     ]
-    for copy in text_copies + image_copies:
+    for copy in image_copies:
         copy.start()
 
     pair = 12.0 * lax.dot_general(
@@ -173,46 +179,50 @@
             total = total + col_in[k - 1, g]
         return total
 
-    image_acc[...] = jnp.zeros_like(image_acc)
-
-    def grad_step(g, own_col):
+    def twos(shape, g, image_axis):
+        ids_i = lax.broadcasted_iota(jnp.int32, shape, image_axis) - lane * rows
+        ids_t = lax.broadcasted_iota(jnp.int32, shape, 1 - image_axis)
+        ids_t = ids_t - (block - g * per_group) * rows
+        return jnp.where((ids_t == ids_i) & (ids_i >= 0) & (ids_i < rows), 2.0, 0.0)
+
+    def there(index, count, k):
+        return pl.ds(pl.multiple_of(lax.rem(index + k, count) * rows, rows), rows)
+
+    def text_step(g, own_col):
         total = col_total(g)
-        col_inv = 1.0 / total
-        col_inv_up = upright(col_inv)
-        first = block - g * per_group
-        ids_t = lax.broadcasted_iota(jnp.int32, (group, images_n), 0) - first * rows
-        ids_i = lax.broadcasted_iota(jnp.int32, (group, images_n), 1) - lane * rows
-        same_t = (ids_t == ids_i) & (ids_i >= 0) & (ids_i < rows)
-        pull_t = (power_t[g] * (row_inv + col_inv_up) - jnp.where(same_t, 2.0, 0.0)).astype(
-            jnp.bfloat16
-        )
-        part = jnp.dot(pull_t, images[...], preferred_element_type=jnp.float32)
+        pull_t = power_t[g] * (row_inv + upright(1.0 / total)) - twos((group, images_n), g, 1)
+        part = jnp.dot(pull_t.astype(jnp.bfloat16), images[...], preferred_element_type=jnp.float32)
         text_own[group_rows(g), :] = part
         text_out[group_rows(g), :] = part.astype(jnp.bfloat16)
-        ids_i = lax.broadcasted_iota(jnp.int32, (images_n, group), 0) - lane * rows
-        ids_t = lax.broadcasted_iota(jnp.int32, (images_n, group), 1) - first * rows
-        same = (ids_t == ids_i) & (ids_i >= 0) & (ids_i < rows)
-        pull = (power[g] * (row_inv_up + col_inv) - jnp.where(same, 2.0, 0.0)).astype(jnp.bfloat16)
-        image_acc[...] += jnp.dot(
-            pull, texts[group_rows(g), :], preferred_element_type=jnp.float32
-        )
-        return own_col + own_piece(total, per_group, first)
-
-    own_col = over_groups(grad_step, jnp.zeros((1, rows), jnp.float32))
-    image_out[...] = image_acc[...].astype(jnp.bfloat16)
-
-    def there(index, count, k):
-        return pl.ds(pl.multiple_of(lax.rem(index + k, count) * rows, rows), rows)
-
+        return own_col + own_piece(total, per_group, block - g * per_group)
+
+    own_col = over_groups(text_step, jnp.zeros((1, rows), jnp.float32))
     tg_copies = [
         to_block(k, text_out.at[there(block, blocks, k)], text_in.at[k - 1], send_tg, recv_tg)
         for k in range(1, blocks)
     ]
+    for copy in tg_copies:
+        copy.start()
+
+    def image_part(g):
+        pull = power[g] * (row_inv_up + 1.0 / col_total(g)) - twos((images_n, group), g, 0)
+        return jnp.dot(
+            pull.astype(jnp.bfloat16), texts[group_rows(g), :], preferred_element_type=jnp.float32
+        )
+
+    image_acc[...] = image_part(0)
+    if groups > 1:
+
+        @pl.loop(1, groups)
+        def _(g):
+            image_acc[...] += image_part(g)
+
+    image_out[...] = image_acc[...].astype(jnp.bfloat16)
     ig_copies = [
         to_lane(k, image_out.at[there(lane, lanes, k)], image_in.at[k - 1], send_ig, recv_ig)
         for k in range(1, lanes)
     ]
-    for copy in tg_copies + ig_copies:
+    for copy in ig_copies:
         copy.start()
     text_loss[...] = jnp.log(own_col) - matched
     for copy in ig_copies:

time: 23.7 us -> 23.3 us (0.983)
  Pallas kernels: 22.9 us -> 22.5 us
    pallas_call x1, Pallas kernels: 22.1 us -> 21.7 us  [body(): pl.pallas_call(functools.partial(kernel, lanes, blocks, group), out_shape...]
where the time goes in v4:
time: 23.3 us; the launch traced here: 23.1 us
  Pallas kernels  22.5 us (97%)
  between operations  0.64 us (3%)
    pallas_call x1, Pallas kernels, body(): pl.pallas_call(functools.partial(kernel, lanes, blocks, group), out_shape...  21.7 us
    pallas_call x1, Pallas kernels, body(): pl.pallas_call(place, out_shape=tuple((jax.ShapeDtypeStruct(r.shape, r.dt...  0.74 us

profile of v4, /device:TPU:0, one launch (start us, length us, event | category | flops | bytes accessed | tf_op | source)
XLA Modules:
  0.0 23.1 jit_solution(11628254547551016413)
XLA Ops:
  0.6 21.7 %shard_map.57 = (f32[1,64]{1,0:T(1,128)S(1)}, f32[1,64]{1,0:T(1,128)S(1)}, f32[64,512]{1,0:T(8,128)S(1)}, f32[64,512]{1,0:T(8,128)S(1)}) custom-call(bf16[64,512]{1,0:T(8,128)(2,1)} %image_hbm.1, bf16[64,512]{1,0:T(8,128)(2,1)} %text_hbm.1), custom_call_target="tpu_custom_call" | custom-call | tf_op jit(solution)/shard_map/pallas_call | solution.py:271
  22.4 0.7 %shard_map.58 = (f32[1,64]{1,0:T(1,128)}, f32[1,64]{1,0:T(1,128)}, f32[64,512]{1,0:T(8,128)}, f32[64,512]{1,0:T(8,128)}) custom-call(f32[1,64]{1,0:T(1,128)S(1)} %get-tuple-element.12.refs_0_, f32[1,64]{1,0:T(1,128)S(1)} %get-tuple-element.13.refs_1_, f32[64,512]{1,0:T(8,128)S(1)} %get-tuple-element.14.refs_2_, f32[64,512]{1,0:T(8,128)S(1)} %get-tuple-element.15.refs_3_), custom_call_target="tpu_custom_call" | custom-call | tf_op jit(solution)/shard_map/pallas_call | solution.py:305

commit v5 on v4

--- a/solution.py
+++ b/solution.py
@@ -231,13 +231,15 @@
     for k in range(1, lanes):
         grad = grad + image_in[k - 1].astype(jnp.float32)
     image_grad[...] = grad
+    for copy in text_copies + image_copies + sum_copies + ig_copies:
+        copy.wait_send()
     for copy in tg_copies:
         copy.wait_recv()
     grad = text_own[my_text, :]
     for k in range(1, blocks):
         grad = grad + text_in[k - 1].astype(jnp.float32)
     text_grad[...] = grad
-    for copy in text_copies + image_copies + sum_copies + tg_copies + ig_copies:
+    for copy in tg_copies:
         copy.wait_send()
 
 

time: 23.3 us -> 23.3 us (level)
  no operation moved by 1% of the time
where the time goes in v5:
time: 23.3 us; the launch traced here: 23.1 us
  Pallas kernels  22.5 us (97%)
  between operations  0.64 us (3%)
    pallas_call x1, Pallas kernels, body(): pl.pallas_call(functools.partial(kernel, lanes, blocks, group), out_shape...  21.7 us
    pallas_call x1, Pallas kernels, body(): pl.pallas_call(place, out_shape=tuple((jax.ShapeDtypeStruct(r.shape, r.dt...  0.74 us

profile of v5, /device:TPU:0, one launch (start us, length us, event | category | flops | bytes accessed | tf_op | source)
XLA Modules:
  0.0 23.1 jit_solution(17758311119677345537)
XLA Ops:
  0.6 21.7 %shard_map.57 = (f32[1,64]{1,0:T(1,128)S(1)}, f32[1,64]{1,0:T(1,128)S(1)}, f32[64,512]{1,0:T(8,128)S(1)}, f32[64,512]{1,0:T(8,128)S(1)}) custom-call(bf16[64,512]{1,0:T(8,128)(2,1)} %image_hbm.1, bf16[64,512]{1,0:T(8,128)(2,1)} %text_hbm.1), custom_call_target="tpu_custom_call" | custom-call | tf_op jit(solution)/shard_map/pallas_call | solution.py:273
  22.4 0.7 %shard_map.58 = (f32[1,64]{1,0:T(1,128)}, f32[1,64]{1,0:T(1,128)}, f32[64,512]{1,0:T(8,128)}, f32[64,512]{1,0:T(8,128)}) custom-call(f32[1,64]{1,0:T(1,128)S(1)} %get-tuple-element.12.refs_0_, f32[1,64]{1,0:T(1,128)S(1)} %get-tuple-element.13.refs_1_, f32[64,512]{1,0:T(8,128)S(1)} %get-tuple-element.14.refs_2_, f32[64,512]{1,0:T(8,128)S(1)} %get-tuple-element.15.refs_3_), custom_call_target="tpu_custom_call" | custom-call | tf_op jit(solution)/shard_map/pallas_call | solution.py:307
